TPU v7x, 32 devices: a whole 2x2x4 slice. The times are simulated.
32 devices in a mesh: groups: 2 (over y), ep: 4 (over x, core), tp: 4 (over z).
Axes of the slice: x: 2, y: 2, z: 4, core: 2. Of those that a mesh axis runs over, the one named last changes fastest.
Arguments:
- tokens: bfloat16 [256, 7168], P(('groups', 'ep')), parts along dimension 0, may hold values from -6 to 6
- w_gate: bfloat16 [16, 7168, 2048], P('ep', None, 'tp'), may hold values from -0.0625 to 0.0625
- w_up: bfloat16 [16, 7168, 2048], P('ep', None, 'tp'), may hold values from -0.0625 to 0.0625
- w_down: bfloat16 [16, 2048, 7168], P('ep', 'tp'), may hold values from -0.1875 to 0.1875
- router_logits: float32 [256, 8], P(('groups', 'ep')), parts along dimension 0, may hold values from -6 to 6
- expert_ids: int32 [256, 8], P(('groups', 'ep')), parts along dimension 0, may hold values from 0 to 15, all different within a row; in each aligned block of 32 rows (0 to 31, 32 to 63, ...) at most 24 rows name the same one
- draft_lengths: int32 [32], P(('groups', 'ep')), parts along dimension 0, may hold values from 7 to 8
- accept_mask: int32 [32, 8], P(('groups', 'ep')), parts along dimension 0, may hold values 0 or 1
Outputs:
- mixed: bfloat16 [256, 7168], P(('groups', 'ep'), 'tp'), parts along dimension 0
- accepted: int32 [2], P('groups'), parts along dimension 0
There are 2 independent parts, one for each index of `groups`. A program takes and returns all parts, laid end to end along the dimension named above; an argument that names none is the same for every part. Nothing has to cross between parts.
Inputs may be any that keep to these rules, and one draw needn't show every extreme that they name: `expert_ids`: each row names 8 different experts. Among the rows of one ep index (aligned blocks of 32 rows) no expert is named by more than 24 rows, and in every draw some expert is named by exactly 24 rows of some block.
All inputs are finite; a program needn't handle non-finite values. No bound on the sum of `accept_mask` on one device may be relied on, other than what follows from the above.
Results may differ from a plain program's by a relative error of at most 0.017.
Values may be sent and summed in bfloat16 or wider, within the bound.
A program may use at most 192 MiB of HBM per device.

v0:
```python
import jax
import jax.numpy as jnp
from jax import lax
from jax.sharding import PartitionSpec as P

DRAFT = 8
EXPERTS = 16


def per_device(tokens, w_gate, w_up, w_down, router_logits, expert_ids, draft_lengths, accept_mask):
    tok_rows = tokens.shape[0]
    local = w_gate.shape[0]
    me = lax.axis_index("ep")
    live = jnp.arange(DRAFT, dtype=jnp.int32)[None, :] < draft_lengths[:, None]
    sig = jax.nn.sigmoid(router_logits)
    gates = 2.827 * sig / jnp.sum(sig, axis=1, keepdims=True)
    named = expert_ids[:, :, None] == jnp.arange(EXPERTS, dtype=jnp.int32)[None, None, :]
    dense = jnp.sum(jnp.where(named, gates[:, :, None], 0.0), axis=1)
    dense = jnp.where(live.reshape(tok_rows)[:, None], dense, 0.0)
    rows = lax.all_gather(tokens, "ep", axis=0, tiled=True)
    dense = lax.all_gather(dense, "ep", axis=0, tiled=True)
    mine = lax.dynamic_slice_in_dim(dense, me * local, local, axis=1)
    gate = jnp.einsum("md,edf->emf", rows, w_gate, preferred_element_type=jnp.float32)
    up = jnp.einsum("md,edf->emf", rows, w_up, preferred_element_type=jnp.float32)
    hidden = (jax.nn.silu(gate) * up * mine.T[:, :, None]).astype(jnp.bfloat16)
    partial = jnp.einsum("emf,efd->md", hidden, w_down, preferred_element_type=jnp.float32)
    partial = partial.astype(jnp.bfloat16)
    partial = lax.psum_scatter(partial, "ep", scatter_dimension=0, tiled=True)
    mixed = lax.psum_scatter(partial, "tp", scatter_dimension=1, tiled=True)
    passed = accept_mask * live.astype(jnp.int32)
    accepted = lax.psum(jnp.sum(jnp.cumprod(passed, axis=1)), "ep").reshape(1)
    return (mixed, accepted)


def solution(mesh):
    placed = (
        P(("groups", "ep"), None),
        P("ep", None, "tp"),
        P("ep", None, "tp"),
        P("ep", "tp", None),
        P(("groups", "ep"), None),
        P(("groups", "ep"), None),
        P(("groups", "ep")),
        P(("groups", "ep"), None),
    )
    return jax.shard_map(
        per_device,
        mesh=mesh,
        in_specs=placed,
        out_specs=(P(("groups", "ep"), "tp"), P("groups")),
        check_vma=False,
    )
```

profile of v0, /device:TPU:0, one launch (start us, length us, event | category | flops | bytes accessed | tf_op | source)
XLA Modules:
  0.0 140.5 jit_solution(3762252298330406964)
XLA Ops:
  7.2 0.0 all-gather.3.cloned.1.call-start
  7.2 0.7 all-gather.3.cloned.1.call-update
  7.9 0.0 reduce-scatter.3.cloned.1.call-start
  7.9 0.7 iota_compare_fusion.1
  8.7 0.1 lt.26
  8.8 0.7 fusion.20
  9.5 0.7 multiply_divide_fusion
  10.2 0.7 select_reduce_fusion
  10.9 6.2 %all-gather = f32[4,32,16]{1,2,0:T(8,128)S(1)} all-gather(f32[1,32,16]{1,2,0:T(8,128)S(1)} %select_bitcast_fusion), channel_id=1, replica_groups=mesh['groups'=2,'ep'=4,'tp'=4] {'ep'}, dimensions={0}, use_global_device_ids=true | all-gather | bytes 10240 | tf_op jit(solution)/shard_map/all_gather | solution.py:21
  17.1 0.1 reshape.28
  17.2 16.2 %all-gather.3.cloned.1.call-done = bf16[128,7168]{1,0:T(8,128)(2,1)} async-done(((bf16[32,7168]{1,0:T(8,128)(2,1)}), bf16[128,7168]{1,0:T(8,128)(2,1)}) %all-gather.3.cloned.1.call-update) | async-done | bytes 1835024 | tf_op jit(solution)/shard_map/all_gather | solution.py:20
  33.4 0.0 copy-start.2
  33.4 17.8 %fusion.5 = f32[4,128,512]{1,2,0:T(8,128)S(1)} fusion(bf16[4,7168,512]{2,1,0:T(8,128)(2,1)} %param.9, bf16[128,7168]{1,0:T(8,128)(2,1)} %all-gather.3.cloned.1.call-done), kind=kOutput, calls=%fused_computation.6 | convolution fusion | flops 3758096384 | bytes 32243712 | tf_op jit(solution)/shard_map/md,edf->emf/dot_general | solution.py:23
  51.2 0.0 copy-done.2
  51.2 0.0 copy-start
  51.2 0.0 copy-start.1
  51.2 14.0 %fusion.17 = bf16[4,128,512]{1,2,0:T(8,128)(2,1)S(1)} fusion(bf16[4,7168,512]{2,1,0:T(8,128)(2,1)} %param.10, bf16[128,7168]{1,0:T(8,128)(2,1)S(1)} %copy-done.2, f32[4,128,512]{1,2,0:T(8,128)S(1)} %fusion.5, f32[4,128]{1,0:T(4,128)S(1)} %dynamic-slice_bitcast_fusion), kind=kOutput, calls=%fused_computation.10 | convolution fusion | flops 3759931392 | bytes 32770048 | tf_op jit(solution)/shard_map/md,edf->emf/dot_general | solution.py:24
  65.2 14.8 %fusion = bf16[128,7168]{1,0:T(8,128)(2,1)} fusion(bf16[4,128,512]{1,2,0:T(8,128)(2,1)S(1)} %fusion.17, bf16[4,512,7168]{2,1,0:T(8,128)(2,1)} %param.11), kind=kOutput, calls=%fused_computation.1 | convolution fusion | flops 3759013888 | bytes 31719424 | tf_op jit(solution)/shard_map/emf,efd->md/dot_general | solution.py:26
  80.0 0.0 reduce-scatter.3.cloned.1.call-update
  80.0 0.0 reduce-scatter.5.cloned.1.call-start
  80.1 29.7 %reduce-scatter.3.cloned.1.call-done = bf16[32,7168]{1,0:T(8,128)(2,1)} async-done(((bf16[128,7168]{1,0:T(8,128)(2,1)}), bf16[32,7168]{1,0:T(8,128)(2,1)}) %reduce-scatter.3.cloned.1.call-update) | async-done | bytes 458768 | tf_op jit(solution)/shard_map/reduce_scatter | solution.py:28
  109.8 0.0 reduce-scatter.5.cloned.1.call-update
  109.8 0.0 copy-done
  109.8 0.0 copy-done.1
  109.8 0.1 broadcast_select_fusion
  109.9 0.2 reduce_window.9
  110.1 0.6 reduce_sum.29
  110.7 4.9 %psum.7 = s32[1]{0:T(128)} all-reduce(s32[1]{0:T(128)} %bitcast.6), channel_id=1, replica_groups=mesh['groups'=2,'ep'=4,'tp'=4] {'ep'}, use_global_device_ids=true, to_apply=%region_6.7 | all-reduce | flops 1 | bytes 8 | tf_op jit(solution)/shard_map/psum | solution.py:31
  115.6 18.4 %reduce-scatter.5.cloned.1.call-done = bf16[32,1792]{1,0:T(8,128)(2,1)} async-done(((bf16[32,7168]{1,0:T(8,128)(2,1)}), bf16[32,1792]{1,0:T(8,128)(2,1)}) %reduce-scatter.5.cloned.1.call-update) | async-done | bytes 114704 | tf_op jit(solution)/shard_map/reduce_scatter | solution.py:29
  (3 shorter events, 0.0 us)
Async XLA Ops:
  7.2 26.2 %all-gather.3.cloned.1.call-start = ((), (), s32[]{:S(2)}) async-start(), calls=%async_computation.2 | async-start | bytes 2293760 | tf_op jit(solution)/shard_map/all_gather | solution.py:20
  7.9 101.9 %reduce-scatter.3.cloned.1.call-start = ((), (), s32[]{:S(2)}) async-start(), calls=%async_computation.3 | async-start | bytes 2293760 | tf_op jit(solution)/shard_map/reduce_scatter | solution.py:28
  33.4 17.8 %copy-start.2 = (bf16[128,7168]{1,0:T(8,128)(2,1)S(1)}, bf16[128,7168]{1,0:T(8,128)(2,1)}, u32[]{:S(2)}) copy-start(bf16[128,7168]{1,0:T(8,128)(2,1)} %all-gather.3.cloned.1.call-done) | copy-start | bytes 5505028
  51.2 58.6 %copy-start = (s32[4,8]{1,0:T(4,128)S(1)}, s32[4,8]{1,0:T(4,128)}, u32[]{:S(2)}) copy-start(s32[4,8]{1,0:T(4,128)} %param.15) | copy-start | bytes 388
  51.2 58.6 %copy-start.1 = (s32[4]{0:T(128)S(1)}, s32[4]{0:T(128)}, u32[]{:S(2)}) copy-start(s32[4]{0:T(128)} %param.14) | copy-start | bytes 52
  80.0 54.0 %reduce-scatter.5.cloned.1.call-start = ((), (), s32[]{:S(2)}) async-start(), calls=%async_computation.4 | async-start | bytes 573440 | tf_op jit(solution)/shard_map/reduce_scatter | solution.py:29
Sparse Core Ops, SparseCore 0:
  9.5 23.8 all-gather.2
  80.2 29.5 reduce-scatter.2
  112.6 21.3 reduce-scatter.4
where the time goes:
time: 141 us
  waiting for transfers between devices  65 us (46%)
  matrix products  46.6 us (33%)
  between operations  13.8 us (10%)
  blocking collectives  11.1 us (8%)
  other arithmetic  3.75 us (3%)
    reduce_scatter x1, waiting for transfers between devices, per_device(): partial = lax.psum_scatter(partial, 'ep', scatter_dimension=0, tiled=True)  29.7 us
    reduce_scatter x1, waiting for transfers between devices, per_device(): mixed = lax.psum_scatter(partial, 'tp', scatter_dimension=1, tiled=True)  18.4 us
    dot_general x1, matrix products, per_device(): jnp.einsum('md,edf->emf', rows, w_gate, preferred_element_type=jnp.float32)  17.8 us
    all_gather x1, waiting for transfers between devices, per_device(): rows = lax.all_gather(tokens, 'ep', axis=0, tiled=True)  16.2 us
    dot_general x1, matrix products, per_device(): jnp.einsum('emf,efd->md', hidden, w_down, preferred_element_type=jnp.floa...  14.8 us
    dot_general x1, matrix products, per_device(): jnp.einsum('md,edf->emf', rows, w_up, preferred_element_type=jnp.float32)  14 us
    all_gather x1, blocking collectives, per_device(): dense = lax.all_gather(dense, 'ep', axis=0, tiled=True)  6.21 us
    psum x1, blocking collectives, per_device(): accepted = lax.psum(jnp.sum(jnp.cumprod(passed, axis=1)), 'ep').reshape(1)  4.89 us
  transfers between devices with their start and end apart: 3, of which 3 were waited for; matrix products, arithmetic and copies ran while one was open for 3% of the time, Pallas kernels for 0%

commit v1 on v0

--- a/solution.py
+++ b/solution.py
@@ -17,8 +17,13 @@
     named = expert_ids[:, :, None] == jnp.arange(EXPERTS, dtype=jnp.int32)[None, None, :]
     dense = jnp.sum(jnp.where(named, gates[:, :, None], 0.0), axis=1)
     dense = jnp.where(live.reshape(tok_rows)[:, None], dense, 0.0)
-    rows = lax.all_gather(tokens, "ep", axis=0, tiled=True)
-    dense = lax.all_gather(dense, "ep", axis=0, tiled=True)
+    rows, dense = jnp.split(
+        lax.all_gather(
+            jnp.concatenate([tokens, dense], axis=1), axis_name="ep", axis=0, tiled=True
+        ),
+        [tokens.shape[1]],
+        axis=1,
+    )
     mine = lax.dynamic_slice_in_dim(dense, me * local, local, axis=1)
     gate = jnp.einsum("md,edf->emf", rows, w_gate, preferred_element_type=jnp.float32)
     up = jnp.einsum("md,edf->emf", rows, w_up, preferred_element_type=jnp.float32)

time: 141 us -> 151 us (1.071)
  waiting for transfers between devices: 65 us -> 82.8 us
  blocking collectives: 11.1 us -> 4.89 us
  matrix products: 46.6 us -> 41.5 us
  other arithmetic: 3.75 us -> 5.88 us
    all_gather x1, waiting for transfers between devices: 16.2 us -> 34.7 us  [per_device(): lax.all_gather(jnp.concatenate([tokens, dense], axis=1), axis_name='ep',...]
    all_gather x1 -> x0, blocking collectives: 6.21 us -> none  [per_device(): dense = lax.all_gather(dense, 'ep', axis=0, tiled=True)]
    dot_general x1, matrix products: 17.8 us -> 12.7 us  [per_device(): jnp.einsum('md,edf->emf', rows, w_gate, preferred_element_type=jnp.float32)]
  transfers between devices with their start and end apart: 3 -> 3, of which waited for: 3 -> 3; matrix products, arithmetic and copies ran while one was open for 3% -> 1% of each run, Pallas kernels for 0% -> 0%
where the time goes in v1:
time: 151 us; the launch traced here: 150 us
  waiting for transfers between devices  82.8 us (55%)
  matrix products  41.5 us (27%)
  between operations  13.8 us (9%)
  other arithmetic  5.88 us (4%)
  blocking collectives  4.89 us (3%)
    all_gather x1, waiting for transfers between devices, per_device(): lax.all_gather(jnp.concatenate([tokens, dense], axis=1), axis_name='ep',...  34.7 us
    reduce_scatter x1, waiting for transfers between devices, per_device(): partial = lax.psum_scatter(partial, 'ep', scatter_dimension=0, tiled=True)  29.7 us
    reduce_scatter x1, waiting for transfers between devices, per_device(): mixed = lax.psum_scatter(partial, 'tp', scatter_dimension=1, tiled=True)  18.4 us
    dot_general x1, matrix products, per_device(): jnp.einsum('emf,efd->md', hidden, w_down, preferred_element_type=jnp.floa...  15.2 us
    dot_general x1, matrix products, per_device(): jnp.einsum('md,edf->emf', rows, w_up, preferred_element_type=jnp.float32)  13.7 us
    dot_general x1, matrix products, per_device(): jnp.einsum('md,edf->emf', rows, w_gate, preferred_element_type=jnp.float32)  12.7 us
    psum x1, blocking collectives, per_device(): accepted = lax.psum(jnp.sum(jnp.cumprod(passed, axis=1)), 'ep').reshape(1)  4.89 us
  transfers between devices with their start and end apart: 3, of which 3 were waited for; matrix products, arithmetic and copies ran while one was open for 1% of the time, Pallas kernels for 0%

profile of v1, /device:TPU:0, one launch (start us, length us, event | category | flops | bytes accessed | tf_op | source)
XLA Modules:
  0.0 150.2 jit_solution(10053839081609812474)
XLA Ops:
  7.2 0.0 all-gather.2.cloned.1.call-start
  7.2 1.1 convert_element_type.10
  8.3 0.7 fusion.8
  9.0 0.7 multiply_divide_fusion
  9.7 0.7 select_reduce_fusion
  10.4 0.1 copy.13
  10.5 0.7 iota_compare_fusion.1
  11.2 0.1 lt.26
  11.3 0.1 broadcast_select_fusion
  11.4 1.0 pad_maximum_fusion
  12.4 0.0 all-gather.2.cloned.1.call-update
  12.4 0.0 reduce-scatter.3.cloned.1.call-start
  12.4 34.7 %all-gather.2.cloned.1.call-done = f32[128,7184]{1,0:T(8,128)} async-done(((f32[32,7184]{1,0:T(8,128)}), f32[128,7184]{1,0:T(8,128)}) %all-gather.2.cloned.1.call-update) | async-done | bytes 3678224 | tf_op jit(solution)/shard_map/all_gather | solution.py:21
  47.1 0.8 split.9
  48.0 0.1 dynamic-slice_bitcast_fusion
  48.0 0.1 copy.14
  48.1 12.7 %fusion.3 = f32[4,128,512]{2,1,0:T(8,128)S(1)} fusion(bf16[4,7168,512]{2,1,0:T(8,128)(2,1)} %param.9, f32[128,7184]{1,0:T(8,128)} %all-gather.2.cloned.1.call-done), kind=kOutput, calls=%fused_computation.5 | convolution fusion | flops 3758096384 | bytes 32243712 | tf_op jit(solution)/shard_map/md,edf->emf/dot_general | solution.py:28
  60.8 0.0 copy-done
  60.8 13.7 %fusion.7 = bf16[4,128,512]{2,1,0:T(8,128)(2,1)S(1)} fusion(bf16[4,7168,512]{2,1,0:T(8,128)(2,1)} %param.10, f32[128,7184]{1,0:T(8,128)S(1)} %copy-done, f32[4,128,512]{2,1,0:T(8,128)S(1)} %fusion.3, f32[4,128]{1,0:T(4,128)S(1)} %copy.14), kind=kOutput, calls=%fused_computation.9 | convolution fusion | flops 3759931392 | bytes 32770048 | tf_op jit(solution)/shard_map/md,edf->emf/dot_general | solution.py:29
  74.5 0.0 copy-start.1
  74.5 0.0 copy-start.2
  74.5 15.2 %fusion = bf16[128,7168]{1,0:T(8,128)(2,1)} fusion(bf16[4,128,512]{2,1,0:T(8,128)(2,1)S(1)} %fusion.7, bf16[4,512,7168]{2,1,0:T(8,128)(2,1)} %param.11), kind=kOutput, calls=%fused_computation.1 | convolution fusion | flops 3759013888 | bytes 31719424 | tf_op jit(solution)/shard_map/emf,efd->md/dot_general | solution.py:31
  89.7 0.0 reduce-scatter.3.cloned.1.call-update
  89.7 0.0 reduce-scatter.5.cloned.1.call-start
  89.7 29.7 %reduce-scatter.3.cloned.1.call-done = bf16[32,7168]{1,0:T(8,128)(2,1)} async-done(((bf16[128,7168]{1,0:T(8,128)(2,1)}), bf16[32,7168]{1,0:T(8,128)(2,1)}) %reduce-scatter.3.cloned.1.call-update) | async-done | bytes 458768 | tf_op jit(solution)/shard_map/reduce_scatter | solution.py:33
  119.4 0.0 reduce-scatter.5.cloned.1.call-update
  119.5 0.0 copy-done.1
  119.5 0.1 broadcast_select_fusion.1
  119.6 0.2 reduce_window.9
  119.7 0.6 reduce_sum.29
  120.4 4.9 %psum.7 = s32[1]{0:T(128)} all-reduce(s32[1]{0:T(128)} %bitcast.5), channel_id=1, replica_groups=mesh['groups'=2,'ep'=4,'tp'=4] {'ep'}, use_global_device_ids=true, to_apply=%region_6.7 | all-reduce | flops 1 | bytes 8 | tf_op jit(solution)/shard_map/psum | solution.py:36
  125.3 18.4 %reduce-scatter.5.cloned.1.call-done = bf16[32,1792]{1,0:T(8,128)(2,1)} async-done(((bf16[32,7168]{1,0:T(8,128)(2,1)}), bf16[32,1792]{1,0:T(8,128)(2,1)}) %reduce-scatter.5.cloned.1.call-update) | async-done | bytes 114704 | tf_op jit(solution)/shard_map/reduce_scatter | solution.py:34
  (2 shorter events, 0.0 us)
Async XLA Ops:
  7.2 40.0 %all-gather.2.cloned.1.call-start = ((), (), s32[]{:S(2)}) async-start(), calls=%async_computation.2 | async-start | bytes 4669440 | tf_op jit(solution)/shard_map/all_gather | solution.py:21
  12.4 107.0 %reduce-scatter.3.cloned.1.call-start = ((), (), s32[]{:S(2)}) async-start(), calls=%async_computation.3 | async-start | bytes 2293760 | tf_op jit(solution)/shard_map/reduce_scatter | solution.py:33
  48.1 12.7 %copy-start = (f32[128,7184]{1,0:T(8,128)S(1)}, f32[128,7184]{1,0:T(8,128)}, u32[]{:S(2)}) copy-start(f32[128,7184]{1,0:T(8,128)} %all-gather.2.cloned.1.call-done) | copy-start | bytes 11034628
  74.5 45.0 %copy-start.1 = (s32[4,8]{1,0:T(4,128)S(1)}, s32[4,8]{1,0:T(4,128)}, u32[]{:S(2)}) copy-start(s32[4,8]{1,0:T(4,128)} %param.15) | copy-start | bytes 388
  74.5 45.0 %copy-start.2 = (s32[4]{0:T(128)S(1)}, s32[4]{0:T(128)}, u32[]{:S(2)}) copy-start(s32[4]{0:T(128)} %param.14) | copy-start | bytes 52
  89.7 54.0 %reduce-scatter.5.cloned.1.call-start = ((), (), s32[]{:S(2)}) async-start(), calls=%async_computation.4 | async-start | bytes 573440 | tf_op jit(solution)/shard_map/reduce_scatter | solution.py:34
Sparse Core Ops, SparseCore 0:
  12.5 34.5 all-gather.1
  89.8 29.5 reduce-scatter.2
  122.3 21.3 reduce-scatter.4
